TPU v7x, 512 devices: a whole 4x8x8 slice. The times are simulated.
512 devices in a mesh: dp: 128 (over z, y, core), mp: 4 (over x).
Axes of the slice: x: 4, y: 8, z: 8, core: 2. Of those that a mesh axis runs over, the one named last changes fastest.
Arguments:
- bag_lengths: int32 [16, 16384], P('mp', 'dp'), may hold values from 1 to 8
- owners: int32 [16, 16384, 8, 1], P('mp', 'dp'), may hold values from 0 to 127; in each aligned block of 1024 rows (0 to 1023, 1024 to 2047, ..., all dimensions but the last counted through in order) at most 16 rows name the same one
- row_slots: int32 [16, 16384, 8], P('mp', 'dp'), may hold values from 0 to 511
- admit_mask: int32 [16, 16384, 8], P('mp', 'dp'), may hold values 0 or 1
- expired: int32 [16, 65536], P('mp', 'dp'), may hold values 0 or 1
- embeddings: float32 [16, 65536, 128], P('mp', 'dp'), may hold values from -3 to 3
- accumulator: float32 [16, 65536], P('mp', 'dp'), may hold values from 0.001 to 0.01
- hidden_weight: bfloat16 [2048, 1024], P(None, 'mp'), may hold values from -0.125 to 0.125
- output_weight: float32 [1024], P('mp'), may hold values from -0.9 to 0.9
- labels: int32 [16384], P('dp'), may hold values 0 or 1
Outputs:
- new_table: float32 [16, 65536, 128], P('mp', 'dp')
- new_accum: float32 [16, 65536], P('mp', 'dp')
- weight_grad: bfloat16 [2048, 1024], P(None, 'mp')
- logits: float32 [16384], P('dp')
Inputs may be any that keep to these rules, and one draw needn't show every extreme that they name: Among the 128 x 8 lookups of one index of dp into one table (aligned blocks of owners' rows), at most 16 name the same owner; in some blocks one owner is named exactly 16 times.
All inputs are finite; a program needn't handle non-finite values. No bound on the sum of `admit_mask` or of `expired` or of `labels` on one device may be relied on, other than what follows from the above.
Results may differ from a plain program's by a relative error of at most 0.0085.
Values may be sent and summed in bfloat16 or wider, within the bound.
No kernel may reach another device: no remote copies, remote signals or barrier semaphores. Data moves between devices by JAX's collectives and lax.ppermute only.
A program may use at most 64 MiB of HBM per device.

v0:
```python
import jax
import jax.numpy as jnp
from jax import lax
from jax.sharding import Mesh
from jax.sharding import PartitionSpec as P

DP = ("dp_0", "dp_1", "dp_2")
LEARN_RATE = 0.05
ACC_RESET = 0.001


def joined_along(parts, dim):
    parts = jnp.moveaxis(parts, 0, dim)
    dims = parts.shape
    return parts.reshape(*dims[:dim], dims[dim] * dims[dim + 1], *dims[dim + 2 :])


def from_everyone(value, axis):
    size = lax.axis_size(axis)
    return lax.all_to_all(
        jnp.broadcast_to(value[None], (size, *value.shape)), axis, 0, 0, tiled=True
    )


def collect_2(value, axis, dim):
    return joined_along(from_everyone(value, axis), dim)


def taken_together(value, axis):
    return from_everyone(value, axis).sum(axis=0)


def cut_along(value, dim, size):
    dims = value.shape
    parts = value.reshape(*dims[:dim], size, dims[dim] // size, *dims[dim + 1 :])
    return jnp.moveaxis(parts, dim, 0)


def summed_on_arrival(value, axis, dim):
    parts = cut_along(value, dim, lax.axis_size(axis))
    arrived = lax.all_to_all(parts, axis, split_axis=0, concat_axis=0, tiled=True)
    return arrived.astype(jnp.float32).sum(axis=0)


def sum_in_two_steps(value, axes, dim):
    far, near = axes
    parts = cut_along(value, dim, lax.axis_size(far))
    nearer = summed_on_arrival(parts, near, dim + 1)
    arrived = lax.all_to_all(
        nearer.astype(jnp.bfloat16), far, split_axis=0, concat_axis=0, tiled=True
    )
    return arrived.astype(jnp.float32).sum(axis=0)


def filled_up(lines, size):
    spare = -lines.shape[0] % size
    if not spare:
        return lines
    return jnp.concatenate([lines, jnp.zeros((spare, *lines.shape[1:]), lines.dtype)])


def gathered_by_axis(value, axes, dim):
    far, near = axes
    parts = from_everyone(from_everyone(value, far), near)
    return joined_along(parts.swapaxes(0, 1).reshape(-1, *value.shape), dim)


def sum_by_parts(value, axes):
    lines = value.reshape(-1, value.shape[-1])
    own = sum_in_two_steps(
        filled_up(lines, lax.axis_size(axes[0]) * lax.axis_size(axes[1])), axes, 0
    )
    whole = gathered_by_axis(own.astype(jnp.bfloat16), axes, 0)
    return whole[: len(lines)].reshape(value.shape).astype(jnp.float32)


def silu_slope(preact):
    sig = jax.nn.sigmoid(preact)
    return sig * (1.0 + preact * (1.0 - sig))


def shards(
    bag_lengths,
    owners,
    row_slots,
    admit_mask,
    expired,
    embeddings,
    accumulator,
    hidden_weight,
    output_weight,
    labels,
):
    groups = lax.axis_size(DP)
    tab_dev, tok_dev, bag_size = row_slots.shape
    rows_dev = embeddings.shape[1]
    row_width = embeddings.shape[2]
    lookups = tok_dev * bag_size
    capacity = 2 * lookups // groups
    buffer_len = groups * capacity
    places = jnp.arange(bag_size, dtype=jnp.int32)
    live_mask = ((places[None, None, :] < bag_lengths[:, :, None]) & (admit_mask == 1)).astype(
        jnp.float32
    )
    counted = jnp.sum(live_mask, axis=2)
    bag_weight = live_mask / jnp.maximum(counted, 1.0)[:, :, None]
    target = owners[..., 0].reshape(tab_dev, lookups)
    lookup_ids = jnp.arange(lookups, dtype=jnp.int32)
    earlier = lookup_ids[None, :] < lookup_ids[:, None]
    same_owner = target[:, :, None] == target[:, None, :]
    ranked = jnp.sum((same_owner & earlier[None, :, :]).astype(jnp.int32), axis=2)
    placed = target * capacity + ranked
    slot_ids = jnp.arange(buffer_len, dtype=jnp.int32)
    hits = placed[:, :, None] == slot_ids[None, None, :]
    flat_slots = row_slots.reshape(tab_dev, lookups)
    request = jnp.sum(jnp.where(hits, flat_slots[:, :, None], 0), axis=1)
    sample_of = lookup_ids // bag_size
    slot_sample = jnp.sum(jnp.where(hits, sample_of[None, :, None], 0), axis=1)
    flat_weight = bag_weight.reshape(tab_dev, lookups)
    slot_weight = jnp.sum(jnp.where(hits, flat_weight[:, :, None], jnp.float32(0.0)), axis=1)
    pool_matrix = jnp.sum(
        jnp.where(
            hits.reshape(tab_dev, tok_dev, bag_size, buffer_len),
            bag_weight[:, :, :, None],
            jnp.float32(0.0),
        ),
        axis=2,
    )
    request = request.reshape(tab_dev, groups, capacity)
    arrived = lax.all_to_all(request, DP, split_axis=1, concat_axis=1, tiled=True)
    fresh_rows = jnp.where(expired[:, :, None] == 1, jnp.float32(0.0), embeddings)
    fresh_acc = jnp.where(expired == 1, jnp.float32(ACC_RESET), accumulator)
    row_pick = (
        arrived.reshape(tab_dev, buffer_len)[:, :, None]
        == jnp.arange(rows_dev, dtype=jnp.int32)[None, None, :]
    ).astype(jnp.bfloat16)
    fetched = jnp.einsum(
        "tbr,tre->tbe",
        row_pick,
        fresh_rows.astype(jnp.bfloat16),
        preferred_element_type=jnp.float32,
    ).astype(jnp.bfloat16)
    fetched = fetched.reshape(tab_dev, groups, capacity, row_width)
    returned = lax.all_to_all(fetched, DP, split_axis=1, concat_axis=1, tiled=True)
    returned_rows = returned.reshape(tab_dev, buffer_len, row_width).astype(jnp.float32)
    pooled = jnp.einsum("tnb,tbe->tne", pool_matrix, returned_rows, precision=lax.Precision.HIGHEST)
    features = pooled.transpose(1, 0, 2).reshape(tok_dev, tab_dev * row_width).astype(jnp.bfloat16)
    portion = collect_2(features, "mp", 1)
    summed_pre = jnp.dot(portion, hidden_weight, preferred_element_type=jnp.float32)
    hidden = jax.nn.silu(summed_pre).astype(jnp.bfloat16)
    logits = taken_together(jnp.sum(hidden.astype(jnp.float32) * output_weight, axis=1), "mp")
    dlogit = jax.nn.sigmoid(logits) - labels.astype(jnp.float32)
    dhidden = (dlogit[:, None] * output_weight * silu_slope(summed_pre)).astype(jnp.bfloat16)
    feature_grad = summed_on_arrival(
        lax.dot_general(
            hidden_weight, dhidden, (((1,), (1,)), ((), ())), preferred_element_type=jnp.float32
        ).astype(jnp.bfloat16),
        "mp",
        0,
    )
    per_table = feature_grad.reshape(tab_dev, row_width, tok_dev).transpose(0, 2, 1)
    sample_pick = (
        slot_sample[:, :, None] == jnp.arange(tok_dev, dtype=jnp.int32)[None, None, :]
    ).astype(jnp.float32)
    slot_grad = jnp.einsum("tbn,tne->tbe", sample_pick, per_table, precision=lax.Precision.HIGHEST)
    outgoing = (slot_weight[:, :, None] * slot_grad).astype(jnp.bfloat16)
    outgoing = outgoing.reshape(tab_dev, groups, capacity, row_width)
    grad_part = lax.all_to_all(outgoing, DP, split_axis=1, concat_axis=1, tiled=True)
    slot_part = lax.all_to_all(request, DP, split_axis=1, concat_axis=1, tiled=True)
    items = grad_part.shape[0]
    selector = (
        slot_part.reshape(items, -1)[:, :, None] == jnp.arange(rows_dev, dtype=jnp.int32)
    ).astype(jnp.bfloat16)
    summed = jnp.einsum(
        "ksr,kse->kre",
        selector,
        grad_part.reshape(items, -1, row_width),
        preferred_element_type=jnp.float32,
    )
    new_acc = fresh_acc + jnp.mean(summed * summed, axis=2)
    new_rows = fresh_rows - LEARN_RATE * summed / jnp.sqrt(new_acc)[:, :, None]
    local_grad = lax.dot_general(
        portion, dhidden, (((0,), (0,)), ((), ())), preferred_element_type=jnp.float32
    )
    weight_grad = sum_by_parts(local_grad.astype(jnp.bfloat16), (("dp_0", "dp_1"), "dp_2")).astype(
        jnp.bfloat16
    )
    return (new_rows, new_acc, weight_grad, logits)


def solution(mesh):
    split = Mesh(mesh.devices.reshape(8, 8, 2, mesh.shape["mp"]), ("dp_0", "dp_1", "dp_2", "mp"))
    return jax.shard_map(
        shards,
        mesh=split,
        in_specs=(
            P("mp", DP),
            P("mp", DP, None, None),
            P("mp", DP, None),
            P("mp", DP, None),
            P("mp", DP),
            P("mp", DP, None),
            P("mp", DP),
            P(None, "mp"),
            P("mp"),
            P(DP),
        ),
        out_specs=(P("mp", DP, None), P("mp", DP), P(None, "mp"), P(DP)),
        check_vma=False,
    )
```

profile of v0, /device:TPU:8, one launch (start us, length us, event | category | flops | bytes accessed | tf_op | source)
XLA Modules:
  0.0 286.2 jit_solution(5932102573414470503)
XLA Ops:
  2.1 3.6 %convert_reduce_fusion = s32[4,1024]{1,0:T(4,128)S(1)} fusion(s32[4,1024]{1,0:T(4,128)S(1)} %reshape_squeeze.3, pred[1024,1024]{1,0:T(8,128)(4,1)S(1)} %iota_compare_fusion.6), kind=kLoop, calls=%fused_computation.9 | loop fusion | flops 16773120 | bytes 1081344 | tf_op jit(solution)/shard_map/reduce_sum | solution.py:111
  6.7 11.5 %select_reduce_fusion.1 = (s32[4,2048]{1,0:T(4,128)S(1)}, s32[4,2048]{1,0:T(4,128)S(1)}) fusion(s32[1024]{0:T(1024)S(1)} %add_select_fusion, s32[4,1024]{1,0:T(4,128)S(1)} %multiply_add_fusion, s32[4,1024]{1,0:T(4,128)S(1)} %broadcast_in_dim.76), kind=kLoop, calls=%fused_computation.2 | loop fusion | flops 41926656 | bytes 102400 | tf_op jit(solution)/shard_map/reduce_sum | solution.py:118
  19.3 17.8 %all-to-all-start = ((s32[4,128,16]{2,0,1:T(4,128)}), s32[4,128,16]{2,0,1:T(4,128)}, u32[]{:S(2)}, u32[]{:S(2)}) async-start(s32[4,128,16]{2,0,1:T(4,128)} %copy.97), calls=%async_computation | async-start | bytes 524288 | tf_op jit(solution)/shard_map/all_to_all | solution.py:169
  37.5 13.9 %all-to-all-done = s32[4,128,16]{2,0,1:T(4,128)} async-done(((s32[4,128,16]{2,0,1:T(4,128)}), s32[4,128,16]{2,0,1:T(4,128)}, u32[]{:S(2)}, u32[]{:S(2)}) %all-to-all-start) | async-done | bytes 32800 | tf_op jit(solution)/shard_map/all_to_all | solution.py:169
  51.4 1.0 copy.98
  52.5 3.3 %fusion.5 = bf16[4,2048,128]{2,1,0:T(8,128)(2,1)S(1)} fusion(s32[4,2048]{1,0:T(4,128)S(1)} %eq.91, f32[4,512,128]{1,2,0:T(8,128)S(1)} %copy.94, pred[4,512]{1,0:T(4,128)(4,1)S(1)} %broadcast_compare_fusion), kind=kOutput, calls=%fused_computation.16 | convolution fusion | flops 1079246848 | bytes 3180544 | tf_op jit(solution)/shard_map/tbr,tre->tbe/dot_general | solution.py:137
  55.9 2.0 copy.103
  57.9 6.1 %all-to-all-start.1 = ((bf16[4,128,16,128]{3,2,0,1:T(8,128)(2,1)}), bf16[4,128,16,128]{3,2,0,1:T(8,128)(2,1)S(1)}, u32[]{:S(2)}, u32[]{:S(2)}) async-start(bf16[4,128,16,128]{3,2,0,1:T(8,128)(2,1)} %copy.103), calls=%async_computation.1 | async-start | bytes 4194304 | tf_op jit(solution)/shard_map/all_to_all | solution.py:144
  65.1 1.1 bitcast_add_fusion
  66.2 12.9 %select_reduce_fusion = f32[4,128,2048]{2,1,0:T(8,128)} fusion(f32[4,128,8]{2,1,0:T(8,128)S(1)} %copy.99, s32[4,128,8]{2,1,0:T(8,128)S(1)} %bitcast_add_fusion), kind=kLoop, calls=%fused_computation | loop fusion | flops 24117248 | bytes 4227072 | tf_op jit(solution)/shard_map/reduce_sum | solution.py:121
  79.1 39.1 %all-to-all-done.1 = bf16[4,128,16,128]{3,2,0,1:T(8,128)(2,1)S(1)} async-done(((bf16[4,128,16,128]{3,2,0,1:T(8,128)(2,1)}), bf16[4,128,16,128]{3,2,0,1:T(8,128)(2,1)S(1)}, u32[]{:S(2)}, u32[]{:S(2)}) %all-to-all-start.1) | async-done | bytes 2097184 | tf_op jit(solution)/shard_map/all_to_all | solution.py:144
  118.5 1.8 copy-done.1
  120.3 2.5 convolution_convert_fusion.2
  122.9 12.9 %all_to_all.52 = bf16[4,128,512]{1,2,0:T(8,128)(2,1)S(1)} all-to-all(bf16[4,128,512]{1,2,0:T(8,128)(2,1)S(1)} %broadcast_in_dim.121), channel_id=1, replica_groups=mesh['dp_0'=8,'dp_1'=8,'dp_2'=2,'mp'=4] {'mp'}, dimensions={0} | all-to-all | bytes 1048576 | tf_op jit(solution)/shard_map/all_to_all | solution.py:20
  136.3 7.6 %all_to_all.53 = f32[4,1,128]{2,1,0:T(1,128)S(1)} all-to-all(f32[4,1,128]{2,1,0:T(1,128)S(1)} %broadcast_in_dim.122), channel_id=1, replica_groups=mesh['dp_0'=8,'dp_1'=8,'dp_2'=2,'mp'=4] {'mp'}, dimensions={0} | all-to-all | bytes 4096 | tf_op jit(solution)/shard_map/all_to_all | solution.py:20
  144.5 4.6 %all_to_all.54 = bf16[2,64,16,256]{3,2,1,0:T(8,128)(2,1)S(1)} all-to-all(bf16[2,64,16,256]{3,2,1,0:T(8,128)(2,1)S(1)} %bitcast.40), channel_id=1, replica_groups=mesh['dp_0'=8,'dp_1'=8,'dp_2'=2,'mp'=4] {'dp_2'}, dimensions={0} | all-to-all | bytes 2097152 | tf_op jit(solution)/shard_map/all_to_all | solution.py:41
  149.1 1.1 reduce_sum.127
  150.2 6.2 %all-to-all-start.7 = ((bf16[64,16,256]{2,1,0:T(8,128)(2,1)}), bf16[64,16,256]{2,1,0:T(8,128)(2,1)S(1)}, u32[]{:S(2)}, u32[]{:S(2)}) async-start(bf16[64,16,256]{2,1,0:T(8,128)(2,1)} %reduce_sum.127), calls=%async_computation.7 | async-start | bytes 1048576 | tf_op jit(solution)/shard_map/all_to_all | solution.py:49
  157.8 18.2 %all-to-all-done.7 = bf16[64,16,256]{2,1,0:T(8,128)(2,1)S(1)} async-done(((bf16[64,16,256]{2,1,0:T(8,128)(2,1)}), bf16[64,16,256]{2,1,0:T(8,128)(2,1)S(1)}, u32[]{:S(2)}, u32[]{:S(2)}) %all-to-all-start.7) | async-done | bytes 524320 | tf_op jit(solution)/shard_map/all_to_all | solution.py:49
  175.9 3.5 %all-to-all-start.4 = ((bf16[4,512,128]{1,2,0:T(8,128)(2,1)}), bf16[4,512,128]{1,2,0:T(8,128)(2,1)S(1)}, u32[]{:S(2)}, u32[]{:S(2)}) async-start(bf16[4,512,128]{1,2,0:T(8,128)(2,1)} %bitcast.37), calls=%async_computation.4 | async-start | bytes 1048576 | tf_op jit(solution)/shard_map/all_to_all | solution.py:41
  179.7 7.8 %all-to-all-done.4 = bf16[4,512,128]{1,2,0:T(8,128)(2,1)S(1)} async-done(((bf16[4,512,128]{1,2,0:T(8,128)(2,1)}), bf16[4,512,128]{1,2,0:T(8,128)(2,1)S(1)}, u32[]{:S(2)}, u32[]{:S(2)}) %all-to-all-start.4) | async-done | bytes 524320 | tf_op jit(solution)/shard_map/all_to_all | solution.py:41
  188.3 6.7 %all-to-all-start.8 = ((bf16[64,16,256]{2,1,0:T(8,128)(2,1)}), bf16[64,16,256]{2,1,0:T(8,128)(2,1)S(1)}, u32[]{:S(2)}, u32[]{:S(2)}) async-start(bf16[64,16,256]{2,1,0:T(8,128)(2,1)} %broadcast_in_dim.124), calls=%async_computation.8 | async-start | bytes 1048576 | tf_op jit(solution)/shard_map/all_to_all | solution.py:20
  195.0 4.9 %select_reduce_fusion.2 = f32[4,2048]{1,0:T(4,128)S(1)} fusion(f32[4,1024]{1,0:T(4,128)S(1)} %broadcast_in_dim.115, s32[4,1024]{1,0:T(4,128)S(1)} %multiply_add_fusion), kind=kLoop, calls=%fused_computation.3 | loop fusion | flops 25157632 | bytes 65536 | tf_op jit(solution)/shard_map/reduce_sum | solution.py:120
  200.2 3.8 %multiply_convert_fusion = bf16[4,2048,128]{2,1,0:T(8,128)(2,1)S(1)} fusion(f32[4,128,128]{2,1,0:T(8,128)S(1)} %bitcast.49, s32[4,2048]{1,0:T(4,128)S(1)} %get-tuple-element.28, f32[4,2048]{1,0:T(4,128)S(1)} %select_reduce_fusion.2), kind=kOutput, calls=%fused_computation.12 | convolution fusion | flops 1613758464 | bytes 2424832 | tf_op jit(solution)/shard_map/tbn,tne->tbe/dot_general | solution.py:165
  204.0 2.0 copy.110
  206.0 7.5 %all-to-all-done.8 = bf16[64,16,256]{2,1,0:T(8,128)(2,1)S(1)} async-done(((bf16[64,16,256]{2,1,0:T(8,128)(2,1)}), bf16[64,16,256]{2,1,0:T(8,128)(2,1)S(1)}, u32[]{:S(2)}, u32[]{:S(2)}) %all-to-all-start.8) | async-done | bytes 524320 | tf_op jit(solution)/shard_map/all_to_all | solution.py:20
  213.5 5.4 %all_to_all.55 = bf16[2,64,16,256]{3,2,1,0:T(8,128)(2,1)} all-to-all(bf16[2,64,16,256]{3,2,1,0:T(8,128)(2,1)S(1)} %broadcast_in_dim.125), channel_id=1, replica_groups=mesh['dp_0'=8,'dp_1'=8,'dp_2'=2,'mp'=4] {'dp_2'}, dimensions={0} | all-to-all | bytes 2097152 | tf_op jit(solution)/shard_map/all_to_all | solution.py:20
  218.9 6.1 %all-to-all-start.5 = ((bf16[4,128,16,128]{3,2,0,1:T(8,128)(2,1)}), bf16[4,128,16,128]{3,2,0,1:T(8,128)(2,1)S(1)}, u32[]{:S(2)}, u32[]{:S(2)}) async-start(bf16[4,128,16,128]{3,2,0,1:T(8,128)(2,1)} %copy.110), calls=%async_computation.5 | async-start | bytes 4194304 | tf_op jit(solution)/shard_map/all_to_all | solution.py:168
  225.1 2.3 copy.114
  227.4 51.8 %all-to-all-done.5 = bf16[4,128,16,128]{3,2,0,1:T(8,128)(2,1)S(1)} async-done(((bf16[4,128,16,128]{3,2,0,1:T(8,128)(2,1)}), bf16[4,128,16,128]{3,2,0,1:T(8,128)(2,1)S(1)}, u32[]{:S(2)}, u32[]{:S(2)}) %all-to-all-start.5) | async-done | bytes 2097184 | tf_op jit(solution)/shard_map/all_to_all | solution.py:168
  279.6 4.4 %multiply_reduce_fusion = (f32[4,512]{1,0:T(4,128)S(1)}, f32[4,512,128]{1,2,0:T(8,128)S(1)}) fusion(bf16[4,2048,128]{2,1,0:T(8,128)(2,1)S(1)} %bitcast.41, s32[4,2048]{1,0:T(4,128)S(1)} %eq.91), kind=kOutput, calls=%fused_computation.23 | convolution fusion | flops 1078458368 | bytes 3186688 | tf_op jit(solution)/shard_map/ksr,kse->kre/dot_general | solution.py:174
  284.9 1.3 copy.115
  (61 shorter events, 10.4 us)
Async XLA Ops:
  0.6 135.2 %copy-start = (bf16[2048,256]{1,0:T(8,128)(2,1)S(1)}, bf16[2048,256]{1,0:T(8,128)(2,1)}, u32[]{:S(2)}) copy-start(bf16[2048,256]{1,0:T(8,128)(2,1)} %param.17) | copy-start | bytes 3145732
  0.6 36.4 %copy-start.6 = (s32[4,512]{1,0:T(4,128)S(1)}, s32[4,512]{1,0:T(4,128)}, u32[]{:S(2)}) copy-start(s32[4,512]{1,0:T(4,128)} %param.14) | copy-start | bytes 24580
  0.7 36.5 %copy-start.5 = (f32[4,512,128]{2,1,0:T(8,128)S(1)}, f32[4,512,128]{2,1,0:T(8,128)}, u32[]{:S(2)}) copy-start(f32[4,512,128]{2,1,0:T(8,128)} %param.15) | copy-start | bytes 3145732
  1.9 53.9 %copy-start.4 = (s32[4,128,8,1]{2,1,0,3:T(8,128)}, s32[4,128,8,1]{2,1,0,3:T(8,128)S(1)}, u32[]{:S(2)}) copy-start(s32[4,128,8,1]{2,1,0,3:T(8,128)S(1)} %copy.95) | copy-start | bytes 49156
  19.3 32.2 %all-to-all-start = ((s32[4,128,16]{2,0,1:T(4,128)}), s32[4,128,16]{2,0,1:T(4,128)}, u32[]{:S(2)}, u32[]{:S(2)}) async-start(s32[4,128,16]{2,0,1:T(4,128)} %copy.97), calls=%async_computation | async-start | bytes 524288 | tf_op jit(solution)/shard_map/all_to_all | solution.py:169
  37.5 18.4 %copy-start.2 = (f32[4,512,128]{1,2,0:T(8,128)}, f32[4,512,128]{1,2,0:T(8,128)S(1)}, u32[]{:S(2)}) copy-start(f32[4,512,128]{1,2,0:T(8,128)S(1)} %copy.94) | copy-start | bytes 3145732
  55.9 9.0 %copy-start.7 = (s32[4,128,8]{1,2,0:T(8,128)S(1)}, s32[4,128,8]{1,2,0:T(8,128)}, u32[]{:S(2)}) copy-start(s32[4,128,8]{1,2,0:T(8,128)} %param.13) | copy-start | bytes 49156
  55.9 9.0 %copy-start.10 = (s32[4,128]{1,0:T(4,128)S(1)}, s32[4,128]{1,0:T(4,128)}, u32[]{:S(2)}) copy-start(s32[4,128]{1,0:T(4,128)} %param.10) | copy-start | bytes 6148
  57.9 60.3 %all-to-all-start.1 = ((bf16[4,128,16,128]{3,2,0,1:T(8,128)(2,1)}), bf16[4,128,16,128]{3,2,0,1:T(8,128)(2,1)S(1)}, u32[]{:S(2)}, u32[]{:S(2)}) async-start(bf16[4,128,16,128]{3,2,0,1:T(8,128)(2,1)} %copy.103), calls=%async_computation.1 | async-start | bytes 4194304 | tf_op jit(solution)/shard_map/all_to_all | solution.py:144
  118.2 2.2 copy-start.1
  118.5 17.3 %copy-start.9 = (f32[256]{0:T(256)S(1)}, f32[256]{0:T(256)}, u32[]{:S(2)}) copy-start(f32[256]{0:T(256)} %param.18) | copy-start | bytes 3076
  120.3 23.6 %copy-start.12 = (s32[128]{0:T(128)S(1)}, s32[128]{0:T(128)}, u32[]{:S(2)}) copy-start(s32[128]{0:T(128)} %param.19) | copy-start | bytes 1540
  143.9 6.3 %copy-start.11 = (f32[128]{0:T(128)}, f32[128]{0:T(128)S(1)}, u32[]{:S(2)}) copy-start(f32[128]{0:T(128)S(1)} %reduce_sum.124) | copy-start | bytes 1540
  150.2 25.7 %all-to-all-start.7 = ((bf16[64,16,256]{2,1,0:T(8,128)(2,1)}), bf16[64,16,256]{2,1,0:T(8,128)(2,1)S(1)}, u32[]{:S(2)}, u32[]{:S(2)}) async-start(bf16[64,16,256]{2,1,0:T(8,128)(2,1)} %reduce_sum.127), calls=%async_computation.7 | async-start | bytes 1048576 | tf_op jit(solution)/shard_map/all_to_all | solution.py:49
  175.9 11.5 %all-to-all-start.4 = ((bf16[4,512,128]{1,2,0:T(8,128)(2,1)}), bf16[4,512,128]{1,2,0:T(8,128)(2,1)S(1)}, u32[]{:S(2)}, u32[]{:S(2)}) async-start(bf16[4,512,128]{1,2,0:T(8,128)(2,1)} %bitcast.37), calls=%async_computation.4 | async-start | bytes 1048576 | tf_op jit(solution)/shard_map/all_to_all | solution.py:41
  188.3 25.2 %all-to-all-start.8 = ((bf16[64,16,256]{2,1,0:T(8,128)(2,1)}), bf16[64,16,256]{2,1,0:T(8,128)(2,1)S(1)}, u32[]{:S(2)}, u32[]{:S(2)}) async-start(bf16[64,16,256]{2,1,0:T(8,128)(2,1)} %broadcast_in_dim.124), calls=%async_computation.8 | async-start | bytes 1048576 | tf_op jit(solution)/shard_map/all_to_all | solution.py:20
  218.9 60.3 %all-to-all-start.5 = ((bf16[4,128,16,128]{3,2,0,1:T(8,128)(2,1)}), bf16[4,128,16,128]{3,2,0,1:T(8,128)(2,1)S(1)}, u32[]{:S(2)}, u32[]{:S(2)}) async-start(bf16[4,128,16,128]{3,2,0,1:T(8,128)(2,1)} %copy.110), calls=%async_computation.5 | async-start | bytes 4194304 | tf_op jit(solution)/shard_map/all_to_all | solution.py:168
  279.6 4.4 %copy-start.8 = (f32[4,512]{1,0:T(4,128)S(1)}, f32[4,512]{1,0:T(4,128)}, u32[]{:S(2)}) copy-start(f32[4,512]{1,0:T(4,128)} %param.16) | copy-start | bytes 24580
  279.6 5.0 %copy-start.3 = (f32[4,512,128]{1,2,0:T(8,128)S(1)}, f32[4,512,128]{1,2,0:T(8,128)}, u32[]{:S(2)}) copy-start(f32[4,512,128]{1,2,0:T(8,128)} %copy-done.2) | copy-start | bytes 3145732
where the time goes:
time: 287 us; the launch traced here: 286 us
  waiting for transfers between devices  138 us (48%)
  starting transfers between devices  46.5 us (16%)
  other arithmetic  36.5 us (13%)
  blocking collectives  30.5 us (11%)
  local copies, waits for them, and re-layouts  18 us (6%)
  matrix products  15.4 us (5%)
    all_to_all x1, waiting for transfers between devices, shards(): lax.all_to_all(outgoing, DP, split_axis=1, concat_axis=1, tiled=True)  51.8 us
    all_to_all x1, waiting for transfers between devices, shards(): lax.all_to_all(fetched, DP, split_axis=1, concat_axis=1, tiled=True)  39.1 us
    all_to_all x3, blocking collectives, from_everyone(): lax.all_to_all(jnp.broadcast_to(value[None], (size, *value.shape)), axis,...  25.9 us
    all_to_all x1, waiting for transfers between devices, sum_in_two_steps(): lax.all_to_all(nearer.astype(jnp.bfloat16), far, split_axis=0, concat_axi...  18.2 us
    all_to_all x1, starting transfers between devices, shards(): lax.all_to_all(request, DP, split_axis=1, concat_axis=1, tiled=True)  17.8 us
    all_to_all x1, waiting for transfers between devices, shards(): lax.all_to_all(request, DP, split_axis=1, concat_axis=1, tiled=True)  13.9 us
    reduce_sum x1, other arithmetic, shards(): jnp.sum(jnp.where(hits.reshape(tab_dev, tok_dev, bag_size, buffer_len), b...  12.9 us
    reduce_sum x1, other arithmetic, shards(): slot_sample = jnp.sum(jnp.where(hits, sample_of[None, :, None], 0), axis=1)  11.5 us
  transfers between devices with their start and end apart: 6, of which 6 were waited for; matrix products, arithmetic and copies ran while one was open for 11% of the time, Pallas kernels for 0%

commit v1 on v0

--- a/solution.py
+++ b/solution.py
@@ -141,7 +141,9 @@
         preferred_element_type=jnp.float32,
     ).astype(jnp.bfloat16)
     fetched = fetched.reshape(tab_dev, groups, capacity, row_width)
-    returned = lax.all_to_all(fetched, DP, split_axis=1, concat_axis=1, tiled=True)
+    returned = jnp.concatenate(
+        lax.all_to_all(jnp.stack(jnp.split(fetched, lax.axis_size(DP), axis=1)), DP, 0, 0), axis=1
+    )
     returned_rows = returned.reshape(tab_dev, buffer_len, row_width).astype(jnp.float32)
     pooled = jnp.einsum("tnb,tbe->tne", pool_matrix, returned_rows, precision=lax.Precision.HIGHEST)
     features = pooled.transpose(1, 0, 2).reshape(tok_dev, tab_dev * row_width).astype(jnp.bfloat16)

time: 287 us -> 362 us (1.26)
  local copies, waits for them, and re-layouts: 18 us -> 92.9 us
    unnamed x30 -> x159, local copies, waits for them, and re-layouts: 5.29 us -> 80.9 us
  transfers between devices with their start and end apart: 6 -> 6, of which waited for: 6 -> 6; matrix products, arithmetic and copies ran while one was open for 11% -> 9% of each run, Pallas kernels for 0% -> 0%
where the time goes in v1:
time: 362 us; the launch traced here: 361 us
  waiting for transfers between devices  136 us (38%)
  local copies, waits for them, and re-layouts  92.9 us (26%)
  starting transfers between devices  46.7 us (13%)
  other arithmetic  37.8 us (10%)
  blocking collectives  30.5 us (8%)
  matrix products  15.4 us (4%)
    unnamed x159, local copies, waits for them, and re-layouts  80.9 us
    all_to_all x1, waiting for transfers between devices, shards(): lax.all_to_all(outgoing, DP, split_axis=1, concat_axis=1, tiled=True)  51.8 us
    all_to_all x1, waiting for transfers between devices, shards(): lax.all_to_all(jnp.stack(jnp.split(fetched, lax.axis_size(DP), axis=1)),...  37.1 us
    all_to_all x3, blocking collectives, from_everyone(): lax.all_to_all(jnp.broadcast_to(value[None], (size, *value.shape)), axis,...  25.9 us
    all_to_all x1, waiting for transfers between devices, sum_in_two_steps(): lax.all_to_all(nearer.astype(jnp.bfloat16), far, split_axis=0, concat_axi...  18.2 us
    all_to_all x1, starting transfers between devices, shards(): lax.all_to_all(request, DP, split_axis=1, concat_axis=1, tiled=True)  17.8 us
    reduce_sum x1, other arithmetic, shards(): jnp.sum(jnp.where(hits.reshape(tab_dev, tok_dev, bag_size, buffer_len), b...  14.2 us
    all_to_all x1, waiting for transfers between devices, shards(): lax.all_to_all(request, DP, split_axis=1, concat_axis=1, tiled=True)  13.9 us
  transfers between devices with their start and end apart: 6, of which 6 were waited for; matrix products, arithmetic and copies ran while one was open for 9% of the time, Pallas kernels for 0%

profile of v1, /device:TPU:8, one launch (start us, length us, event | category | flops | bytes accessed | tf_op | source)
XLA Modules:
  0.0 360.6 jit_solution(16491223548534019653)
XLA Ops:
  1.0 0.9 copy.731
  2.1 3.6 convert_reduce_fusion
  6.0 11.5 %select_reduce_fusion.1 = (s32[4,2048]{1,0:T(4,128)S(1)}, s32[4,2048]{1,0:T(4,128)S(1)}) fusion(s32[1024]{0:T(1024)S(1)} %add_select_fusion, s32[4,1024]{1,0:T(4,128)S(1)} %multiply_add_fusion, s32[4,1024]{1,0:T(4,128)S(1)} %broadcast_in_dim.76), kind=kLoop, calls=%fused_computation.2 | loop fusion | flops 41926656 | bytes 102400 | tf_op jit(solution)/shard_map/reduce_sum | solution.py:118
  18.6 17.8 %all-to-all-start = ((s32[4,128,16]{2,0,1:T(4,128)}), s32[4,128,16]{2,0,1:T(4,128)}, u32[]{:S(2)}, u32[]{:S(2)}) async-start(s32[4,128,16]{2,0,1:T(4,128)} %copy.733), calls=%async_computation | async-start | bytes 524288 | tf_op jit(solution)/shard_map/all_to_all | solution.py:171
  36.8 13.9 %all-to-all-done = s32[4,128,16]{2,0,1:T(4,128)} async-done(((s32[4,128,16]{2,0,1:T(4,128)}), s32[4,128,16]{2,0,1:T(4,128)}, u32[]{:S(2)}, u32[]{:S(2)}) %all-to-all-start) | async-done | bytes 32800 | tf_op jit(solution)/shard_map/all_to_all | solution.py:171
  50.7 1.0 copy.734
  51.8 3.3 fusion.5
  132.2 6.3 %all-to-all-start.1 = ((bf16[128,4,1,16,128]{4,3,1,2,0:T(8,128)(2,1)}), bf16[128,4,1,16,128]{4,3,1,2,0:T(8,128)(2,1)S(1)}, u32[]{:S(2)}, u32[]{:S(2)}) async-start(bf16[128,4,1,16,128]{4,3,1,2,0:T(8,128)(2,1)} %constant_dynamic-update-slice_fusion), calls=%async_computation.1 | async-start | bytes 4194304 | tf_op jit(solution)/shard_map/all_to_all | solution.py:145
  140.2 1.0 bitcast_add_fusion
  141.2 14.2 %select_reduce_fusion = f32[4,128,2048]{2,1,0:T(8,128)} fusion(f32[4,128,8]{2,1,0:T(8,128)} %copy.735, s32[4,128,8]{2,1,0:T(8,128)S(1)} %bitcast_add_fusion), kind=kLoop, calls=%fused_computation | loop fusion | flops 24117248 | bytes 4227072 | tf_op jit(solution)/shard_map/reduce_sum | solution.py:121
  155.4 37.1 %all-to-all-done.1 = bf16[128,4,1,16,128]{4,3,1,2,0:T(8,128)(2,1)S(1)} async-done(((bf16[128,4,1,16,128]{4,3,1,2,0:T(8,128)(2,1)}), bf16[128,4,1,16,128]{4,3,1,2,0:T(8,128)(2,1)S(1)}, u32[]{:S(2)}, u32[]{:S(2)}) %all-to-all-start.1) | async-done | bytes 2097184 | tf_op jit(solution)/shard_map/all_to_all | solution.py:145
  192.9 1.8 copy-done.1
  194.8 2.5 convolution_convert_fusion.2
  197.4 12.9 %all_to_all.52 = bf16[4,128,512]{1,2,0:T(8,128)(2,1)S(1)} all-to-all(bf16[4,128,512]{1,2,0:T(8,128)(2,1)S(1)} %broadcast_in_dim.121), channel_id=1, replica_groups=mesh['dp_0'=8,'dp_1'=8,'dp_2'=2,'mp'=4] {'mp'}, dimensions={0} | all-to-all | bytes 1048576 | tf_op jit(solution)/shard_map/all_to_all | solution.py:20
  210.7 7.6 %all_to_all.53 = f32[4,1,128]{2,1,0:T(1,128)S(1)} all-to-all(f32[4,1,128]{2,1,0:T(1,128)S(1)} %broadcast_in_dim.122), channel_id=1, replica_groups=mesh['dp_0'=8,'dp_1'=8,'dp_2'=2,'mp'=4] {'mp'}, dimensions={0} | all-to-all | bytes 4096 | tf_op jit(solution)/shard_map/all_to_all | solution.py:20
  219.0 4.6 %all_to_all.54 = bf16[2,64,16,256]{3,2,1,0:T(8,128)(2,1)S(1)} all-to-all(bf16[2,64,16,256]{3,2,1,0:T(8,128)(2,1)S(1)} %bitcast.810), channel_id=1, replica_groups=mesh['dp_0'=8,'dp_1'=8,'dp_2'=2,'mp'=4] {'dp_2'}, dimensions={0} | all-to-all | bytes 2097152 | tf_op jit(solution)/shard_map/all_to_all | solution.py:41
  223.5 1.1 reduce_sum.127
  224.6 6.3 %all-to-all-start.7 = ((bf16[64,16,256]{2,1,0:T(8,128)(2,1)}), bf16[64,16,256]{2,1,0:T(8,128)(2,1)S(1)}, u32[]{:S(2)}, u32[]{:S(2)}) async-start(bf16[64,16,256]{2,1,0:T(8,128)(2,1)} %reduce_sum.127), calls=%async_computation.7 | async-start | bytes 1048576 | tf_op jit(solution)/shard_map/all_to_all | solution.py:49
  232.2 18.2 %all-to-all-done.7 = bf16[64,16,256]{2,1,0:T(8,128)(2,1)S(1)} async-done(((bf16[64,16,256]{2,1,0:T(8,128)(2,1)}), bf16[64,16,256]{2,1,0:T(8,128)(2,1)S(1)}, u32[]{:S(2)}, u32[]{:S(2)}) %all-to-all-start.7) | async-done | bytes 524320 | tf_op jit(solution)/shard_map/all_to_all | solution.py:49
  250.4 3.5 all-to-all-start.4
  254.1 7.8 %all-to-all-done.4 = bf16[4,512,128]{1,2,0:T(8,128)(2,1)S(1)} async-done(((bf16[4,512,128]{1,2,0:T(8,128)(2,1)}), bf16[4,512,128]{1,2,0:T(8,128)(2,1)S(1)}, u32[]{:S(2)}, u32[]{:S(2)}) %all-to-all-start.4) | async-done | bytes 524320 | tf_op jit(solution)/shard_map/all_to_all | solution.py:41
  262.7 6.7 %all-to-all-start.8 = ((bf16[64,16,256]{2,1,0:T(8,128)(2,1)}), bf16[64,16,256]{2,1,0:T(8,128)(2,1)S(1)}, u32[]{:S(2)}, u32[]{:S(2)}) async-start(bf16[64,16,256]{2,1,0:T(8,128)(2,1)} %broadcast_in_dim.124), calls=%async_computation.8 | async-start | bytes 1048576 | tf_op jit(solution)/shard_map/all_to_all | solution.py:20
  269.5 4.9 %select_reduce_fusion.2 = f32[4,2048]{1,0:T(4,128)S(1)} fusion(f32[4,1024]{1,0:T(4,128)S(1)} %broadcast_in_dim.115, s32[4,1024]{1,0:T(4,128)S(1)} %multiply_add_fusion), kind=kLoop, calls=%fused_computation.3 | loop fusion | flops 25157632 | bytes 65536 | tf_op jit(solution)/shard_map/reduce_sum | solution.py:120
  274.6 3.8 %multiply_convert_fusion = bf16[4,2048,128]{2,1,0:T(8,128)(2,1)S(1)} fusion(f32[4,128,128]{2,1,0:T(8,128)S(1)} %bitcast.946, s32[4,2048]{1,0:T(4,128)S(1)} %get-tuple-element.28, f32[4,2048]{1,0:T(4,128)S(1)} %select_reduce_fusion.2), kind=kOutput, calls=%fused_computation.12 | convolution fusion | flops 1613758464 | bytes 2424832 | tf_op jit(solution)/shard_map/tbn,tne->tbe/dot_general | solution.py:167
  278.4 2.0 copy.873
  280.4 7.5 %all-to-all-done.8 = bf16[64,16,256]{2,1,0:T(8,128)(2,1)S(1)} async-done(((bf16[64,16,256]{2,1,0:T(8,128)(2,1)}), bf16[64,16,256]{2,1,0:T(8,128)(2,1)S(1)}, u32[]{:S(2)}, u32[]{:S(2)}) %all-to-all-start.8) | async-done | bytes 524320 | tf_op jit(solution)/shard_map/all_to_all | solution.py:20
  288.0 5.4 %all_to_all.55 = bf16[2,64,16,256]{3,2,1,0:T(8,128)(2,1)} all-to-all(bf16[2,64,16,256]{3,2,1,0:T(8,128)(2,1)S(1)} %broadcast_in_dim.125), channel_id=1, replica_groups=mesh['dp_0'=8,'dp_1'=8,'dp_2'=2,'mp'=4] {'dp_2'}, dimensions={0} | all-to-all | bytes 2097152 | tf_op jit(solution)/shard_map/all_to_all | solution.py:20
  293.3 6.1 %all-to-all-start.5 = ((bf16[4,128,16,128]{3,2,0,1:T(8,128)(2,1)}), bf16[4,128,16,128]{3,2,0,1:T(8,128)(2,1)S(1)}, u32[]{:S(2)}, u32[]{:S(2)}) async-start(bf16[4,128,16,128]{3,2,0,1:T(8,128)(2,1)} %copy.873), calls=%async_computation.5 | async-start | bytes 4194304 | tf_op jit(solution)/shard_map/all_to_all | solution.py:170
  299.5 2.3 copy.877
  301.8 51.8 %all-to-all-done.5 = bf16[4,128,16,128]{3,2,0,1:T(8,128)(2,1)S(1)} async-done(((bf16[4,128,16,128]{3,2,0,1:T(8,128)(2,1)}), bf16[4,128,16,128]{3,2,0,1:T(8,128)(2,1)S(1)}, u32[]{:S(2)}, u32[]{:S(2)}) %all-to-all-start.5) | async-done | bytes 2097184 | tf_op jit(solution)/shard_map/all_to_all | solution.py:170
  354.0 4.4 %multiply_reduce_fusion = (f32[4,512]{1,0:T(4,128)S(1)}, f32[4,512,128]{1,2,0:T(8,128)S(1)}) fusion(bf16[4,2048,128]{2,1,0:T(8,128)(2,1)S(1)} %bitcast.811, s32[4,2048]{1,0:T(4,128)S(1)} %eq.91), kind=kOutput, calls=%fused_computation.23 | convolution fusion | flops 1078458368 | bytes 3186688 | tf_op jit(solution)/shard_map/ksr,kse->kre/dot_general | solution.py:176
  359.3 1.3 copy.878
  (190 shorter events, 86.4 us)
Async XLA Ops:
  0.6 209.6 %copy-start = (bf16[2048,256]{1,0:T(8,128)(2,1)S(1)}, bf16[2048,256]{1,0:T(8,128)(2,1)}, u32[]{:S(2)}) copy-start(bf16[2048,256]{1,0:T(8,128)(2,1)} %param.17) | copy-start | bytes 3145732
  0.6 5.1 %copy-start.7 = (s32[4,128,8]{1,2,0:T(8,128)S(1)}, s32[4,128,8]{1,2,0:T(8,128)}, u32[]{:S(2)}) copy-start(s32[4,128,8]{1,2,0:T(8,128)} %param.12) | copy-start | bytes 49156
  1.0 35.4 %copy-start.6 = (s32[4,512]{1,0:T(4,128)S(1)}, s32[4,512]{1,0:T(4,128)}, u32[]{:S(2)}) copy-start(s32[4,512]{1,0:T(4,128)} %param.14) | copy-start | bytes 24580
  1.0 35.4 %copy-start.5 = (f32[4,512,128]{2,1,0:T(8,128)S(1)}, f32[4,512,128]{2,1,0:T(8,128)}, u32[]{:S(2)}) copy-start(f32[4,512,128]{2,1,0:T(8,128)} %param.15) | copy-start | bytes 3145732
  18.6 32.2 %all-to-all-start = ((s32[4,128,16]{2,0,1:T(4,128)}), s32[4,128,16]{2,0,1:T(4,128)}, u32[]{:S(2)}, u32[]{:S(2)}) async-start(s32[4,128,16]{2,0,1:T(4,128)} %copy.733), calls=%async_computation | async-start | bytes 524288 | tf_op jit(solution)/shard_map/all_to_all | solution.py:171
  36.8 18.4 %copy-start.2 = (f32[4,512,128]{1,2,0:T(8,128)}, f32[4,512,128]{1,2,0:T(8,128)S(1)}, u32[]{:S(2)}) copy-start(f32[4,512,128]{1,2,0:T(8,128)S(1)} %copy.730) | copy-start | bytes 3145732
  132.2 7.2 %copy-start.8 = (s32[4,128,8]{1,2,0:T(8,128)S(1)}, s32[4,128,8]{1,2,0:T(8,128)}, u32[]{:S(2)}) copy-start(s32[4,128,8]{1,2,0:T(8,128)} %param.13) | copy-start | bytes 49156
  132.2 7.2 %copy-start.11 = (s32[4,128]{1,0:T(4,128)S(1)}, s32[4,128]{1,0:T(4,128)}, u32[]{:S(2)}) copy-start(s32[4,128]{1,0:T(4,128)} %param.10) | copy-start | bytes 6148
  132.2 60.4 %all-to-all-start.1 = ((bf16[128,4,1,16,128]{4,3,1,2,0:T(8,128)(2,1)}), bf16[128,4,1,16,128]{4,3,1,2,0:T(8,128)(2,1)S(1)}, u32[]{:S(2)}, u32[]{:S(2)}) async-start(bf16[128,4,1,16,128]{4,3,1,2,0:T(8,128)(2,1)} %constant_dynamic-update-slice_fusion), calls=%async_computation.1 | async-start | bytes 4194304 | tf_op jit(solution)/shard_map/all_to_all | solution.py:145
  192.6 2.2 copy-start.1
  194.8 15.5 %copy-start.10 = (f32[256]{0:T(256)S(1)}, f32[256]{0:T(256)}, u32[]{:S(2)}) copy-start(f32[256]{0:T(256)} %param.18) | copy-start | bytes 3076
  197.3 21.1 %copy-start.13 = (s32[128]{0:T(128)S(1)}, s32[128]{0:T(128)}, u32[]{:S(2)}) copy-start(s32[128]{0:T(128)} %param.19) | copy-start | bytes 1540
  218.3 5.2 %copy-start.12 = (f32[128]{0:T(128)}, f32[128]{0:T(128)S(1)}, u32[]{:S(2)}) copy-start(f32[128]{0:T(128)S(1)} %reduce_sum.124) | copy-start | bytes 1540
  224.6 25.7 %all-to-all-start.7 = ((bf16[64,16,256]{2,1,0:T(8,128)(2,1)}), bf16[64,16,256]{2,1,0:T(8,128)(2,1)S(1)}, u32[]{:S(2)}, u32[]{:S(2)}) async-start(bf16[64,16,256]{2,1,0:T(8,128)(2,1)} %reduce_sum.127), calls=%async_computation.7 | async-start | bytes 1048576 | tf_op jit(solution)/shard_map/all_to_all | solution.py:49
  230.9 23.0 %copy-start.4 = (f32[4,128,8]{2,1,0:T(8,128)S(1)}, f32[4,128,8]{2,1,0:T(8,128)}, u32[]{:S(2)}) copy-start(f32[4,128,8]{2,1,0:T(8,128)} %copy.735) | copy-start | bytes 49156
  250.4 11.5 %all-to-all-start.4 = ((bf16[4,512,128]{1,2,0:T(8,128)(2,1)}), bf16[4,512,128]{1,2,0:T(8,128)(2,1)S(1)}, u32[]{:S(2)}, u32[]{:S(2)}) async-start(bf16[4,512,128]{1,2,0:T(8,128)(2,1)} %bitcast.807), calls=%async_computation.4 | async-start | bytes 1048576 | tf_op jit(solution)/shard_map/all_to_all | solution.py:41
  262.7 25.2 %all-to-all-start.8 = ((bf16[64,16,256]{2,1,0:T(8,128)(2,1)}), bf16[64,16,256]{2,1,0:T(8,128)(2,1)S(1)}, u32[]{:S(2)}, u32[]{:S(2)}) async-start(bf16[64,16,256]{2,1,0:T(8,128)(2,1)} %broadcast_in_dim.124), calls=%async_computation.8 | async-start | bytes 1048576 | tf_op jit(solution)/shard_map/all_to_all | solution.py:20
  293.3 60.3 %all-to-all-start.5 = ((bf16[4,128,16,128]{3,2,0,1:T(8,128)(2,1)}), bf16[4,128,16,128]{3,2,0,1:T(8,128)(2,1)S(1)}, u32[]{:S(2)}, u32[]{:S(2)}) async-start(bf16[4,128,16,128]{3,2,0,1:T(8,128)(2,1)} %copy.873), calls=%async_computation.5 | async-start | bytes 4194304 | tf_op jit(solution)/shard_map/all_to_all | solution.py:170
  354.0 4.4 %copy-start.9 = (f32[4,512]{1,0:T(4,128)S(1)}, f32[4,512]{1,0:T(4,128)}, u32[]{:S(2)}) copy-start(f32[4,512]{1,0:T(4,128)} %param.16) | copy-start | bytes 24580
  354.0 5.0 %copy-start.3 = (f32[4,512,128]{1,2,0:T(8,128)S(1)}, f32[4,512,128]{1,2,0:T(8,128)}, u32[]{:S(2)}) copy-start(f32[4,512,128]{1,2,0:T(8,128)} %copy-done.2) | copy-start | bytes 3145732
